TPU v7x, 32 devices: a whole 2x2x4 slice. The times are simulated.
32 devices in a mesh: level: 4 (over x, core), space: 8 (over z, y).
Axes of the slice: x: 2, y: 2, z: 4, core: 2. Of those that a mesh axis runs over, the one named last changes fastest.
Arguments:
- u_init: float32 [256, 2048], P('space'), may hold values from 0.2 to 1
- v_init: float32 [256, 2048], P('space'), may hold values from 0 to 0.5
- feed_rate: float32 [256, 2048], P('space'), may hold values from 0.01 to 0.12
- kill_rate: float32 [256, 2048], P('space'), may hold values from 0.02 to 0.16
Outputs:
- level_states: float32 [4, 2, 256, 2048], P('level', None, 'space')
All inputs are finite; a program needn't handle non-finite values.
Results may differ from a plain program's by a relative error of at most 0.0003.
Values sent between devices are 32-bit elements; how exact they have to be, the bound alone decides.
A program may use at most 64 MiB of HBM per device.

v0:
```python
import jax
import jax.numpy as jnp
from jax import lax
from jax.sharding import PartitionSpec as P

STEPS = 4
SWEEPS = 3


time_step = 1.0
diffusion = (1.0, 0.5)
quad_weights = [
    [9.0, 19.0, -5.0, 1.0, 0.0],
    [-1.0, 13.0, 13.0, -1.0, 0.0],
    [1.0, -5.0, 19.0, 9.0, 0.0],
    [0.0, 1.0, -5.0, 19.0, 9.0],
]


def padded_2(block, sides, width):
    for axis, dim in sides:
        count = lax.axis_size(axis)
        forward = [(i, i + 1) for i in range(count - 1)]
        forward.append((count - 1, 0))
        backward = [(target, source) for source, target in forward]
        low = lax.ppermute(
            lax.slice_in_dim(block, block.shape[dim] - width, None, axis=dim), axis, forward
        )
        high = lax.ppermute(lax.slice_in_dim(block, 0, width, axis=dim), axis, backward)
        block = jnp.concatenate([low, block, high], axis=dim)
    return block


def from_behind(block, axis, distance):
    devices = range(lax.axis_size(axis))
    route = [(i - distance, i) for i in devices if i - distance in devices]
    return lax.ppermute(block, axis, route)


def reaction(state, feed_rate, kill_rate):
    u_field = state[0]
    v_field = state[1]
    uv_square = u_field * v_field * v_field
    return jnp.stack(
        [-uv_square + feed_rate * (1.0 - u_field), uv_square - (feed_rate + kill_rate) * v_field]
    )


def around_sum(padded):
    middle = padded[:, 1:-1]
    return padded[:, :-2] + padded[:, 2:] + jnp.roll(middle, 1, 2) + jnp.roll(middle, -1, 2)


def edge_laplace(padded, rate_field):
    return rate_field * (around_sum(padded) - 4.0 * padded[:, 1:-1])


def jacobi_sweep(padded, source, step_rate):
    return (source + step_rate * around_sum(padded)) / (1.0 + 4.0 * step_rate)


def jacobi_solve(source, extra_rim, step_rate):
    widened = padded_2(source, (("space", 1),), SWEEPS + extra_rim)
    wide_rows = widened.shape[1]
    iterate = widened
    for sweep_idx in range(SWEEPS):
        iterate = jacobi_sweep(
            iterate, widened[:, sweep_idx + 1 : wide_rows - sweep_idx - 1], step_rate
        )
    return iterate


def store_node(buffer, value, node_idx, usable):
    former = lax.dynamic_index_in_dim(buffer, node_idx, 0, keepdims=False)
    return lax.dynamic_update_index_in_dim(buffer, jnp.where(usable, value, former), node_idx, 0)


def run_relay(u_init, v_init, feed_rate, kill_rate, weight_table, rate_field, step_rate):
    initial = jnp.stack([u_init, v_init])
    levels = lax.axis_size("level")
    level_idx = lax.axis_index("level")
    upper_flag = (level_idx > 0).astype(jnp.float32)
    start_pad = padded_2(initial, (("space", 1),), 1)
    blank_buf = jnp.zeros((STEPS + 1,) + initial.shape, jnp.float32)
    lap_buf = blank_buf.at[0].set(edge_laplace(start_pad, rate_field))
    rea_buf = blank_buf.at[0].set(reaction(initial, feed_rate, kill_rate))
    extra_rim = 0

    def advance(tick_idx, loop_state):
        state, lap_buf, rea_buf = loop_state
        offset = tick_idx - 3 * level_idx
        active = (offset >= 0) & (offset < STEPS)
        step_idx = jnp.clip(offset, 0, STEPS - 1)
        weights = lax.dynamic_index_in_dim(weight_table, step_idx, 0, keepdims=False)
        quadrature = time_step * jnp.einsum(
            "m,mfij->fij", weights, lap_buf + rea_buf, precision=lax.Precision.HIGHEST
        )
        lap_next = lax.dynamic_index_in_dim(lap_buf, step_idx + 1, 0, keepdims=False)
        rea_now = lax.dynamic_index_in_dim(rea_buf, step_idx, 0, keepdims=False)
        correction = quadrature - time_step * lap_next - time_step * rea_now
        source = state + time_step * reaction(state, feed_rate, kill_rate) + upper_flag * correction
        solved = jacobi_solve(source, extra_rim, step_rate)
        new_state = jnp.where(active, solved, state)
        received = from_behind(new_state, "level", 1)
        received_pad = padded_2(received, (("space", 1),), 1)
        received_lap = edge_laplace(received_pad, rate_field)
        received_rea = reaction(received, feed_rate, kill_rate)
        node_raw = offset + 4
        usable = (node_raw >= 1) & (node_raw <= STEPS) & (level_idx > 0)
        node_idx = jnp.clip(node_raw, 0, STEPS)
        lap_buf = store_node(lap_buf, received_lap, node_idx, usable)
        rea_buf = store_node(rea_buf, received_rea, node_idx, usable)
        return (new_state, lap_buf, rea_buf)

    tick_count = STEPS + 3 * (levels - 1)
    final_state, lap_done, rea_done = lax.fori_loop(
        0, tick_count, advance, (initial, lap_buf, rea_buf)
    )
    return final_state[None]


def body(u_init, v_init, feed_rate, kill_rate):
    weight_table = jnp.array(quad_weights, jnp.float32) / 24.0
    rate_field = jnp.array(diffusion, jnp.float32)[:, None, None]
    step_rate = time_step * rate_field
    return run_relay(u_init, v_init, feed_rate, kill_rate, weight_table, rate_field, step_rate)


def solution(mesh):
    return jax.shard_map(
        body,
        mesh=mesh,
        in_specs=(P("space", None), P("space", None), P("space", None), P("space", None)),
        out_specs=P("level", None, "space", None),
        check_vma=False,
    )
```

profile of v0, /device:TPU:2, one launch (start us, length us, event | category | flops | bytes accessed | tf_op | source)
XLA Modules:
  0.0 551.1 jit_solution(13055936773437660624)
XLA Ops:
  2.6 3.2 collective-permute-start.6
  16.5 534.6 %while.23 = (s32[]{:T(128)}, f32[2,32,2048]{2,1,0:T(8,128)}, f32[5,2,32,2048]{3,2,1,0:T(8,128)}, f32[5,2,32,2048]{3,2,1,0:T(8,128)S(1)}, s32[]{:T(128)}, /*index...) while((s32[]{:T(128)}, f32[2,32,2048]{2,1,0:T(8,128)}, ...), condition=%wide.region_1.2_spmd.clone, body=%wide.region_0.1_spmd.clone.sunk | while | flops 16433175 | bytes 46661028 | solution.py:116
  18.8 6.2 %fusion.82 = f32[1,2,32,2048]{3,0,2,1:T(1,128)S(1)} fusion(f32[5,2,32,2048]{3,2,1,0:T(8,128)S(1)} %add.594, f32[4,5]{1,0:T(4,128)} %get-tuple-element.534, s32[]{:T(128)S(6)} %min.27), kind=kOutput, calls=%fused_computation.1.clone.1 | convolution fusion | flops 7864320 | bytes 3146244 | tf_op jit(solution)/shard_map/while/body/eval_jaxpr/m,mfij->fij/dot_general | solution.py:95
  30.5 2.4 collective-permute-done
  32.9 4.6 collective-permute-done.1
  44.3 7.7 %collective-permute-done.2 = f32[2,32,2048]{2,1,0:T(8,128)S(1)} collective-permute-done((f32[2,32,2048]{2,1,0:T(8,128)}, f32[2,32,2048]{2,1,0:T(8,128)S(1)}, u32[]{:S(2)}, u32[]{:S(2)}) %collective-permute-start.2) | collective-permute-done | bytes 524320 | tf_op jit(solution)/shard_map/while/body/eval_jaxpr/ppermute | solution.py:37
  55.8 2.8 collective-permute-done.4
  61.9 6.2 %fusion.82 = f32[1,2,32,2048]{3,0,2,1:T(1,128)S(1)} fusion(f32[5,2,32,2048]{3,2,1,0:T(8,128)S(1)} %add.594, f32[4,5]{1,0:T(4,128)} %get-tuple-element.534, s32[]{:T(128)S(6)} %min.27), kind=kOutput, calls=%fused_computation.1.clone.1 | convolution fusion | flops 7864320 | bytes 3146244 | tf_op jit(solution)/shard_map/while/body/eval_jaxpr/m,mfij->fij/dot_general | solution.py:95
  73.6 2.4 collective-permute-done
  76.1 2.7 collective-permute-done.1
  85.6 7.7 %collective-permute-done.2 = f32[2,32,2048]{2,1,0:T(8,128)S(1)} collective-permute-done((f32[2,32,2048]{2,1,0:T(8,128)}, f32[2,32,2048]{2,1,0:T(8,128)S(1)}, u32[]{:S(2)}, u32[]{:S(2)}) %collective-permute-start.2) | collective-permute-done | bytes 524320 | tf_op jit(solution)/shard_map/while/body/eval_jaxpr/ppermute | solution.py:37
  97.1 2.8 collective-permute-done.4
  103.2 6.2 %fusion.82 = f32[1,2,32,2048]{3,0,2,1:T(1,128)S(1)} fusion(f32[5,2,32,2048]{3,2,1,0:T(8,128)S(1)} %add.594, f32[4,5]{1,0:T(4,128)} %get-tuple-element.534, s32[]{:T(128)S(6)} %min.27), kind=kOutput, calls=%fused_computation.1.clone.1 | convolution fusion | flops 7864320 | bytes 3146244 | tf_op jit(solution)/shard_map/while/body/eval_jaxpr/m,mfij->fij/dot_general | solution.py:95
  114.9 2.4 collective-permute-done
  117.4 2.7 collective-permute-done.1
  126.9 7.7 %collective-permute-done.2 = f32[2,32,2048]{2,1,0:T(8,128)S(1)} collective-permute-done((f32[2,32,2048]{2,1,0:T(8,128)}, f32[2,32,2048]{2,1,0:T(8,128)S(1)}, u32[]{:S(2)}, u32[]{:S(2)}) %collective-permute-start.2) | collective-permute-done | bytes 524320 | tf_op jit(solution)/shard_map/while/body/eval_jaxpr/ppermute | solution.py:37
  138.4 2.8 collective-permute-done.4
  144.5 6.2 %fusion.82 = f32[1,2,32,2048]{3,0,2,1:T(1,128)S(1)} fusion(f32[5,2,32,2048]{3,2,1,0:T(8,128)S(1)} %add.594, f32[4,5]{1,0:T(4,128)} %get-tuple-element.534, s32[]{:T(128)S(6)} %min.27), kind=kOutput, calls=%fused_computation.1.clone.1 | convolution fusion | flops 7864320 | bytes 3146244 | tf_op jit(solution)/shard_map/while/body/eval_jaxpr/m,mfij->fij/dot_general | solution.py:95
  156.2 2.4 collective-permute-done
  158.7 2.7 collective-permute-done.1
  168.2 7.7 %collective-permute-done.2 = f32[2,32,2048]{2,1,0:T(8,128)S(1)} collective-permute-done((f32[2,32,2048]{2,1,0:T(8,128)}, f32[2,32,2048]{2,1,0:T(8,128)S(1)}, u32[]{:S(2)}, u32[]{:S(2)}) %collective-permute-start.2) | collective-permute-done | bytes 524320 | tf_op jit(solution)/shard_map/while/body/eval_jaxpr/ppermute | solution.py:37
  179.7 2.8 collective-permute-done.4
  185.8 6.2 %fusion.82 = f32[1,2,32,2048]{3,0,2,1:T(1,128)S(1)} fusion(f32[5,2,32,2048]{3,2,1,0:T(8,128)S(1)} %add.594, f32[4,5]{1,0:T(4,128)} %get-tuple-element.534, s32[]{:T(128)S(6)} %min.27), kind=kOutput, calls=%fused_computation.1.clone.1 | convolution fusion | flops 7864320 | bytes 3146244 | tf_op jit(solution)/shard_map/while/body/eval_jaxpr/m,mfij->fij/dot_general | solution.py:95
  197.5 2.4 collective-permute-done
  200.0 2.7 collective-permute-done.1
  209.5 7.7 %collective-permute-done.2 = f32[2,32,2048]{2,1,0:T(8,128)S(1)} collective-permute-done((f32[2,32,2048]{2,1,0:T(8,128)}, f32[2,32,2048]{2,1,0:T(8,128)S(1)}, u32[]{:S(2)}, u32[]{:S(2)}) %collective-permute-start.2) | collective-permute-done | bytes 524320 | tf_op jit(solution)/shard_map/while/body/eval_jaxpr/ppermute | solution.py:37
  221.0 2.8 collective-permute-done.4
  227.1 6.2 %fusion.82 = f32[1,2,32,2048]{3,0,2,1:T(1,128)S(1)} fusion(f32[5,2,32,2048]{3,2,1,0:T(8,128)S(1)} %add.594, f32[4,5]{1,0:T(4,128)} %get-tuple-element.534, s32[]{:T(128)S(6)} %min.27), kind=kOutput, calls=%fused_computation.1.clone.1 | convolution fusion | flops 7864320 | bytes 3146244 | tf_op jit(solution)/shard_map/while/body/eval_jaxpr/m,mfij->fij/dot_general | solution.py:95
  238.8 2.4 collective-permute-done
  241.3 2.7 collective-permute-done.1
  250.8 7.7 %collective-permute-done.2 = f32[2,32,2048]{2,1,0:T(8,128)S(1)} collective-permute-done((f32[2,32,2048]{2,1,0:T(8,128)}, f32[2,32,2048]{2,1,0:T(8,128)S(1)}, u32[]{:S(2)}, u32[]{:S(2)}) %collective-permute-start.2) | collective-permute-done | bytes 524320 | tf_op jit(solution)/shard_map/while/body/eval_jaxpr/ppermute | solution.py:37
  262.3 2.8 collective-permute-done.4
  268.4 6.2 %fusion.82 = f32[1,2,32,2048]{3,0,2,1:T(1,128)S(1)} fusion(f32[5,2,32,2048]{3,2,1,0:T(8,128)S(1)} %add.594, f32[4,5]{1,0:T(4,128)} %get-tuple-element.534, s32[]{:T(128)S(6)} %min.27), kind=kOutput, calls=%fused_computation.1.clone.1 | convolution fusion | flops 7864320 | bytes 3146244 | tf_op jit(solution)/shard_map/while/body/eval_jaxpr/m,mfij->fij/dot_general | solution.py:95
  280.1 2.4 collective-permute-done
  282.5 2.7 collective-permute-done.1
  291.1 7.7 %collective-permute-done.2 = f32[2,32,2048]{2,1,0:T(8,128)S(1)} collective-permute-done((f32[2,32,2048]{2,1,0:T(8,128)}, f32[2,32,2048]{2,1,0:T(8,128)S(1)}, u32[]{:S(2)}, u32[]{:S(2)}) %collective-permute-start.2) | collective-permute-done | bytes 524320 | tf_op jit(solution)/shard_map/while/body/eval_jaxpr/ppermute | solution.py:37
  302.6 2.8 collective-permute-done.4
  308.7 6.2 %fusion.82 = f32[1,2,32,2048]{3,0,2,1:T(1,128)S(1)} fusion(f32[5,2,32,2048]{3,2,1,0:T(8,128)S(1)} %add.594, f32[4,5]{1,0:T(4,128)} %get-tuple-element.534, s32[]{:T(128)S(6)} %min.27), kind=kOutput, calls=%fused_computation.1.clone.1 | convolution fusion | flops 7864320 | bytes 3146244 | tf_op jit(solution)/shard_map/while/body/eval_jaxpr/m,mfij->fij/dot_general | solution.py:95
  320.4 2.4 collective-permute-done
  322.8 2.7 collective-permute-done.1
  331.3 7.7 %collective-permute-done.2 = f32[2,32,2048]{2,1,0:T(8,128)S(1)} collective-permute-done((f32[2,32,2048]{2,1,0:T(8,128)}, f32[2,32,2048]{2,1,0:T(8,128)S(1)}, u32[]{:S(2)}, u32[]{:S(2)}) %collective-permute-start.2) | collective-permute-done | bytes 524320 | tf_op jit(solution)/shard_map/while/body/eval_jaxpr/ppermute | solution.py:37
  342.8 2.8 collective-permute-done.4
  348.9 6.2 %fusion.82 = f32[1,2,32,2048]{3,0,2,1:T(1,128)S(1)} fusion(f32[5,2,32,2048]{3,2,1,0:T(8,128)S(1)} %add.594, f32[4,5]{1,0:T(4,128)} %get-tuple-element.534, s32[]{:T(128)S(6)} %min.27), kind=kOutput, calls=%fused_computation.1.clone.1 | convolution fusion | flops 7864320 | bytes 3146244 | tf_op jit(solution)/shard_map/while/body/eval_jaxpr/m,mfij->fij/dot_general | solution.py:95
  360.6 2.4 collective-permute-done
  363.1 2.7 collective-permute-done.1
  371.6 7.7 %collective-permute-done.2 = f32[2,32,2048]{2,1,0:T(8,128)S(1)} collective-permute-done((f32[2,32,2048]{2,1,0:T(8,128)}, f32[2,32,2048]{2,1,0:T(8,128)S(1)}, u32[]{:S(2)}, u32[]{:S(2)}) %collective-permute-start.2) | collective-permute-done | bytes 524320 | tf_op jit(solution)/shard_map/while/body/eval_jaxpr/ppermute | solution.py:37
  383.1 2.8 collective-permute-done.4
  389.2 6.2 %fusion.82 = f32[1,2,32,2048]{3,0,2,1:T(1,128)S(1)} fusion(f32[5,2,32,2048]{3,2,1,0:T(8,128)S(1)} %add.594, f32[4,5]{1,0:T(4,128)} %get-tuple-element.534, s32[]{:T(128)S(6)} %min.27), kind=kOutput, calls=%fused_computation.1.clone.1 | convolution fusion | flops 7864320 | bytes 3146244 | tf_op jit(solution)/shard_map/while/body/eval_jaxpr/m,mfij->fij/dot_general | solution.py:95
  403.3 2.7 collective-permute-done.1
  411.9 7.7 %collective-permute-done.2 = f32[2,32,2048]{2,1,0:T(8,128)S(1)} collective-permute-done((f32[2,32,2048]{2,1,0:T(8,128)}, f32[2,32,2048]{2,1,0:T(8,128)S(1)}, u32[]{:S(2)}, u32[]{:S(2)}) %collective-permute-start.2) | collective-permute-done | bytes 524320 | tf_op jit(solution)/shard_map/while/body/eval_jaxpr/ppermute | solution.py:37
  423.4 2.8 collective-permute-done.4
  429.4 6.2 %fusion.82 = f32[1,2,32,2048]{3,0,2,1:T(1,128)S(1)} fusion(f32[5,2,32,2048]{3,2,1,0:T(8,128)S(1)} %add.594, f32[4,5]{1,0:T(4,128)} %get-tuple-element.534, s32[]{:T(128)S(6)} %min.27), kind=kOutput, calls=%fused_computation.1.clone.1 | convolution fusion | flops 7864320 | bytes 3146244 | tf_op jit(solution)/shard_map/while/body/eval_jaxpr/m,mfij->fij/dot_general | solution.py:95
  441.1 2.4 collective-permute-done
  443.6 2.7 collective-permute-done.1
  453.2 7.7 %collective-permute-done.2 = f32[2,32,2048]{2,1,0:T(8,128)S(1)} collective-permute-done((f32[2,32,2048]{2,1,0:T(8,128)}, f32[2,32,2048]{2,1,0:T(8,128)S(1)}, u32[]{:S(2)}, u32[]{:S(2)}) %collective-permute-start.2) | collective-permute-done | bytes 524320 | tf_op jit(solution)/shard_map/while/body/eval_jaxpr/ppermute | solution.py:37
  464.7 2.8 collective-permute-done.4
  470.7 6.2 %fusion.82 = f32[1,2,32,2048]{3,0,2,1:T(1,128)S(1)} fusion(f32[5,2,32,2048]{3,2,1,0:T(8,128)S(1)} %add.594, f32[4,5]{1,0:T(4,128)} %get-tuple-element.534, s32[]{:T(128)S(6)} %min.27), kind=kOutput, calls=%fused_computation.1.clone.1 | convolution fusion | flops 7864320 | bytes 3146244 | tf_op jit(solution)/shard_map/while/body/eval_jaxpr/m,mfij->fij/dot_general | solution.py:95
  484.9 2.7 collective-permute-done.1
  494.5 7.7 %collective-permute-done.2 = f32[2,32,2048]{2,1,0:T(8,128)S(1)} collective-permute-done((f32[2,32,2048]{2,1,0:T(8,128)}, f32[2,32,2048]{2,1,0:T(8,128)S(1)}, u32[]{:S(2)}, u32[]{:S(2)}) %collective-permute-start.2) | collective-permute-done | bytes 524320 | tf_op jit(solution)/shard_map/while/body/eval_jaxpr/ppermute | solution.py:37
  506.0 2.8 collective-permute-done.4
  512.0 6.2 %fusion.82 = f32[1,2,32,2048]{3,0,2,1:T(1,128)S(1)} fusion(f32[5,2,32,2048]{3,2,1,0:T(8,128)S(1)} %add.594, f32[4,5]{1,0:T(4,128)} %get-tuple-element.534, s32[]{:T(128)S(6)} %min.27), kind=kOutput, calls=%fused_computation.1.clone.1 | convolution fusion | flops 7864320 | bytes 3146244 | tf_op jit(solution)/shard_map/while/body/eval_jaxpr/m,mfij->fij/dot_general | solution.py:95
  526.2 2.7 collective-permute-done.1
  535.8 7.7 %collective-permute-done.2 = f32[2,32,2048]{2,1,0:T(8,128)S(1)} collective-permute-done((f32[2,32,2048]{2,1,0:T(8,128)}, f32[2,32,2048]{2,1,0:T(8,128)S(1)}, u32[]{:S(2)}, u32[]{:S(2)}) %collective-permute-start.2) | collective-permute-done | bytes 524320 | tf_op jit(solution)/shard_map/while/body/eval_jaxpr/ppermute | solution.py:37
  547.3 2.8 collective-permute-done.4
  (375 shorter events, 268.3 us)
Async XLA Ops:
  1.0 11.4 %collective-permute-start.5 = (f32[2,1,2048]{2,1,0:T(1,128)S(1)}, f32[2,1,2048]{2,1,0:T(1,128)S(1)}, u32[]{:S(2)}, u32[]{:S(2)}) collective-permute-start(f32[2,1,2048]{2,1,0:T(1,128)S(1)} %get-tuple-element.387), channel_id=1, source_target_pairs={{0,1},{1,2},{2,3},{3,4},{4,5},{5,6},{6,7},{7,0},{8,9},{9,10},{10,1... | collective-permute-start | bytes 49160 | tf_op jit(solution)/shard_map/ppermute | solution.py:26
  2.6 9.8 %collective-permute-start.6 = (f32[2,1,2048]{2,1,0:T(1,128)S(1)}, f32[2,1,2048]{2,1,0:T(1,128)S(1)}, u32[]{:S(2)}, u32[]{:S(2)}) collective-permute-start(f32[2,1,2048]{2,1,0:T(1,128)S(1)} %get-tuple-element.388), channel_id=1, source_target_pairs={{1,0},{2,1},{3,2},{4,3},{5,4},{6,5},{7,6},{0,7},{9,8},{10,9},{11,1... | collective-permute-start | bytes 49160 | tf_op jit(solution)/shard_map/ppermute | solution.py:29
  28.4 4.5 collective-permute-start
  30.3 7.2 %collective-permute-start.1 = (f32[2,3,2048]{2,1,0:T(4,128)}, f32[2,3,2048]{2,1,0:T(4,128)S(1)}, u32[]{:S(2)}, u32[]{:S(2)}) collective-permute-start(f32[2,3,2048]{2,1,0:T(4,128)} %get-tuple-element.475), channel_id=1, source_target_pairs={{0,1},{1,2},{2,3},{3,4},{4,5},{5,6},{6,7},{7,0},{8,9},{9,10},{10,1... | collective-permute-start | bytes 147464 | tf_op jit(solution)/shard_map/while/body/eval_jaxpr/ppermute | solution.py:26
  41.3 10.7 %collective-permute-start.2 = (f32[2,32,2048]{2,1,0:T(8,128)}, f32[2,32,2048]{2,1,0:T(8,128)S(1)}, u32[]{:S(2)}, u32[]{:S(2)}) collective-permute-start(f32[2,32,2048]{2,1,0:T(8,128)} %fusion.92), channel_id=1, source_target_pairs={{0,8},{8,16},{16,24},{1,9},{9,17},{17,25},{2,10},{10,18},{18,26},{... | collective-permute-start | bytes 1572872 | tf_op jit(solution)/shard_map/while/body/eval_jaxpr/ppermute | solution.py:37
  52.0 3.8 collective-permute-start.3
  52.1 6.5 %collective-permute-start.4 = (f32[2,1,2048]{2,1,0:T(1,128)S(1)}, f32[2,1,2048]{2,1,0:T(1,128)S(1)}, u32[]{:S(2)}, u32[]{:S(2)}) collective-permute-start(f32[2,1,2048]{2,1,0:T(1,128)S(1)} %get-tuple-element.487), channel_id=1, source_target_pairs={{0,1},{1,2},{2,3},{3,4},{4,5},{5,6},{6,7},{7,0},{8,9},{9,10},{10,1... | collective-permute-start | bytes 49160 | tf_op jit(solution)/shard_map/while/body/eval_jaxpr/ppermute | solution.py:26
  71.6 4.5 collective-permute-start
  71.6 7.2 %collective-permute-start.1 = (f32[2,3,2048]{2,1,0:T(4,128)}, f32[2,3,2048]{2,1,0:T(4,128)S(1)}, u32[]{:S(2)}, u32[]{:S(2)}) collective-permute-start(f32[2,3,2048]{2,1,0:T(4,128)} %get-tuple-element.475), channel_id=1, source_target_pairs={{0,1},{1,2},{2,3},{3,4},{4,5},{5,6},{6,7},{7,0},{8,9},{9,10},{10,1... | collective-permute-start | bytes 147464 | tf_op jit(solution)/shard_map/while/body/eval_jaxpr/ppermute | solution.py:26
  82.6 10.7 %collective-permute-start.2 = (f32[2,32,2048]{2,1,0:T(8,128)}, f32[2,32,2048]{2,1,0:T(8,128)S(1)}, u32[]{:S(2)}, u32[]{:S(2)}) collective-permute-start(f32[2,32,2048]{2,1,0:T(8,128)} %fusion.92), channel_id=1, source_target_pairs={{0,8},{8,16},{16,24},{1,9},{9,17},{17,25},{2,10},{10,18},{18,26},{... | collective-permute-start | bytes 1572872 | tf_op jit(solution)/shard_map/while/body/eval_jaxpr/ppermute | solution.py:37
  93.3 3.8 collective-permute-start.3
  93.4 6.5 %collective-permute-start.4 = (f32[2,1,2048]{2,1,0:T(1,128)S(1)}, f32[2,1,2048]{2,1,0:T(1,128)S(1)}, u32[]{:S(2)}, u32[]{:S(2)}) collective-permute-start(f32[2,1,2048]{2,1,0:T(1,128)S(1)} %get-tuple-element.487), channel_id=1, source_target_pairs={{0,1},{1,2},{2,3},{3,4},{4,5},{5,6},{6,7},{7,0},{8,9},{9,10},{10,1... | collective-permute-start | bytes 49160 | tf_op jit(solution)/shard_map/while/body/eval_jaxpr/ppermute | solution.py:26
  112.9 4.5 collective-permute-start
  112.9 7.2 %collective-permute-start.1 = (f32[2,3,2048]{2,1,0:T(4,128)}, f32[2,3,2048]{2,1,0:T(4,128)S(1)}, u32[]{:S(2)}, u32[]{:S(2)}) collective-permute-start(f32[2,3,2048]{2,1,0:T(4,128)} %get-tuple-element.475), channel_id=1, source_target_pairs={{0,1},{1,2},{2,3},{3,4},{4,5},{5,6},{6,7},{7,0},{8,9},{9,10},{10,1... | collective-permute-start | bytes 147464 | tf_op jit(solution)/shard_map/while/body/eval_jaxpr/ppermute | solution.py:26
  123.9 10.7 %collective-permute-start.2 = (f32[2,32,2048]{2,1,0:T(8,128)}, f32[2,32,2048]{2,1,0:T(8,128)S(1)}, u32[]{:S(2)}, u32[]{:S(2)}) collective-permute-start(f32[2,32,2048]{2,1,0:T(8,128)} %fusion.92), channel_id=1, source_target_pairs={{0,8},{8,16},{16,24},{1,9},{9,17},{17,25},{2,10},{10,18},{18,26},{... | collective-permute-start | bytes 1572872 | tf_op jit(solution)/shard_map/while/body/eval_jaxpr/ppermute | solution.py:37
  134.6 3.8 collective-permute-start.3
  134.7 6.5 %collective-permute-start.4 = (f32[2,1,2048]{2,1,0:T(1,128)S(1)}, f32[2,1,2048]{2,1,0:T(1,128)S(1)}, u32[]{:S(2)}, u32[]{:S(2)}) collective-permute-start(f32[2,1,2048]{2,1,0:T(1,128)S(1)} %get-tuple-element.487), channel_id=1, source_target_pairs={{0,1},{1,2},{2,3},{3,4},{4,5},{5,6},{6,7},{7,0},{8,9},{9,10},{10,1... | collective-permute-start | bytes 49160 | tf_op jit(solution)/shard_map/while/body/eval_jaxpr/ppermute | solution.py:26
  154.2 4.5 collective-permute-start
  154.2 7.2 %collective-permute-start.1 = (f32[2,3,2048]{2,1,0:T(4,128)}, f32[2,3,2048]{2,1,0:T(4,128)S(1)}, u32[]{:S(2)}, u32[]{:S(2)}) collective-permute-start(f32[2,3,2048]{2,1,0:T(4,128)} %get-tuple-element.475), channel_id=1, source_target_pairs={{0,1},{1,2},{2,3},{3,4},{4,5},{5,6},{6,7},{7,0},{8,9},{9,10},{10,1... | collective-permute-start | bytes 147464 | tf_op jit(solution)/shard_map/while/body/eval_jaxpr/ppermute | solution.py:26
  165.2 10.7 %collective-permute-start.2 = (f32[2,32,2048]{2,1,0:T(8,128)}, f32[2,32,2048]{2,1,0:T(8,128)S(1)}, u32[]{:S(2)}, u32[]{:S(2)}) collective-permute-start(f32[2,32,2048]{2,1,0:T(8,128)} %fusion.92), channel_id=1, source_target_pairs={{0,8},{8,16},{16,24},{1,9},{9,17},{17,25},{2,10},{10,18},{18,26},{... | collective-permute-start | bytes 1572872 | tf_op jit(solution)/shard_map/while/body/eval_jaxpr/ppermute | solution.py:37
  175.9 3.8 collective-permute-start.3
  176.0 6.5 %collective-permute-start.4 = (f32[2,1,2048]{2,1,0:T(1,128)S(1)}, f32[2,1,2048]{2,1,0:T(1,128)S(1)}, u32[]{:S(2)}, u32[]{:S(2)}) collective-permute-start(f32[2,1,2048]{2,1,0:T(1,128)S(1)} %get-tuple-element.487), channel_id=1, source_target_pairs={{0,1},{1,2},{2,3},{3,4},{4,5},{5,6},{6,7},{7,0},{8,9},{9,10},{10,1... | collective-permute-start | bytes 49160 | tf_op jit(solution)/shard_map/while/body/eval_jaxpr/ppermute | solution.py:26
  195.5 4.5 collective-permute-start
  195.5 7.2 %collective-permute-start.1 = (f32[2,3,2048]{2,1,0:T(4,128)}, f32[2,3,2048]{2,1,0:T(4,128)S(1)}, u32[]{:S(2)}, u32[]{:S(2)}) collective-permute-start(f32[2,3,2048]{2,1,0:T(4,128)} %get-tuple-element.475), channel_id=1, source_target_pairs={{0,1},{1,2},{2,3},{3,4},{4,5},{5,6},{6,7},{7,0},{8,9},{9,10},{10,1... | collective-permute-start | bytes 147464 | tf_op jit(solution)/shard_map/while/body/eval_jaxpr/ppermute | solution.py:26
  206.5 10.7 %collective-permute-start.2 = (f32[2,32,2048]{2,1,0:T(8,128)}, f32[2,32,2048]{2,1,0:T(8,128)S(1)}, u32[]{:S(2)}, u32[]{:S(2)}) collective-permute-start(f32[2,32,2048]{2,1,0:T(8,128)} %fusion.92), channel_id=1, source_target_pairs={{0,8},{8,16},{16,24},{1,9},{9,17},{17,25},{2,10},{10,18},{18,26},{... | collective-permute-start | bytes 1572872 | tf_op jit(solution)/shard_map/while/body/eval_jaxpr/ppermute | solution.py:37
  217.3 3.8 collective-permute-start.3
  217.3 6.5 %collective-permute-start.4 = (f32[2,1,2048]{2,1,0:T(1,128)S(1)}, f32[2,1,2048]{2,1,0:T(1,128)S(1)}, u32[]{:S(2)}, u32[]{:S(2)}) collective-permute-start(f32[2,1,2048]{2,1,0:T(1,128)S(1)} %get-tuple-element.487), channel_id=1, source_target_pairs={{0,1},{1,2},{2,3},{3,4},{4,5},{5,6},{6,7},{7,0},{8,9},{9,10},{10,1... | collective-permute-start | bytes 49160 | tf_op jit(solution)/shard_map/while/body/eval_jaxpr/ppermute | solution.py:26
  236.8 4.5 collective-permute-start
  236.8 7.2 %collective-permute-start.1 = (f32[2,3,2048]{2,1,0:T(4,128)}, f32[2,3,2048]{2,1,0:T(4,128)S(1)}, u32[]{:S(2)}, u32[]{:S(2)}) collective-permute-start(f32[2,3,2048]{2,1,0:T(4,128)} %get-tuple-element.475), channel_id=1, source_target_pairs={{0,1},{1,2},{2,3},{3,4},{4,5},{5,6},{6,7},{7,0},{8,9},{9,10},{10,1... | collective-permute-start | bytes 147464 | tf_op jit(solution)/shard_map/while/body/eval_jaxpr/ppermute | solution.py:26
  247.8 10.7 %collective-permute-start.2 = (f32[2,32,2048]{2,1,0:T(8,128)}, f32[2,32,2048]{2,1,0:T(8,128)S(1)}, u32[]{:S(2)}, u32[]{:S(2)}) collective-permute-start(f32[2,32,2048]{2,1,0:T(8,128)} %fusion.92), channel_id=1, source_target_pairs={{0,8},{8,16},{16,24},{1,9},{9,17},{17,25},{2,10},{10,18},{18,26},{... | collective-permute-start | bytes 1572872 | tf_op jit(solution)/shard_map/while/body/eval_jaxpr/ppermute | solution.py:37
  258.5 3.8 collective-permute-start.3
  258.6 6.5 %collective-permute-start.4 = (f32[2,1,2048]{2,1,0:T(1,128)S(1)}, f32[2,1,2048]{2,1,0:T(1,128)S(1)}, u32[]{:S(2)}, u32[]{:S(2)}) collective-permute-start(f32[2,1,2048]{2,1,0:T(1,128)S(1)} %get-tuple-element.487), channel_id=1, source_target_pairs={{0,1},{1,2},{2,3},{3,4},{4,5},{5,6},{6,7},{7,0},{8,9},{9,10},{10,1... | collective-permute-start | bytes 49160 | tf_op jit(solution)/shard_map/while/body/eval_jaxpr/ppermute | solution.py:26
  278.1 4.5 collective-permute-start
  278.1 7.2 %collective-permute-start.1 = (f32[2,3,2048]{2,1,0:T(4,128)}, f32[2,3,2048]{2,1,0:T(4,128)S(1)}, u32[]{:S(2)}, u32[]{:S(2)}) collective-permute-start(f32[2,3,2048]{2,1,0:T(4,128)} %get-tuple-element.475), channel_id=1, source_target_pairs={{0,1},{1,2},{2,3},{3,4},{4,5},{5,6},{6,7},{7,0},{8,9},{9,10},{10,1... | collective-permute-start | bytes 147464 | tf_op jit(solution)/shard_map/while/body/eval_jaxpr/ppermute | solution.py:26
  288.1 10.7 %collective-permute-start.2 = (f32[2,32,2048]{2,1,0:T(8,128)}, f32[2,32,2048]{2,1,0:T(8,128)S(1)}, u32[]{:S(2)}, u32[]{:S(2)}) collective-permute-start(f32[2,32,2048]{2,1,0:T(8,128)} %fusion.92), channel_id=1, source_target_pairs={{0,8},{8,16},{16,24},{1,9},{9,17},{17,25},{2,10},{10,18},{18,26},{... | collective-permute-start | bytes 1572872 | tf_op jit(solution)/shard_map/while/body/eval_jaxpr/ppermute | solution.py:37
  298.8 3.8 collective-permute-start.3
  298.8 6.5 %collective-permute-start.4 = (f32[2,1,2048]{2,1,0:T(1,128)S(1)}, f32[2,1,2048]{2,1,0:T(1,128)S(1)}, u32[]{:S(2)}, u32[]{:S(2)}) collective-permute-start(f32[2,1,2048]{2,1,0:T(1,128)S(1)} %get-tuple-element.487), channel_id=1, source_target_pairs={{0,1},{1,2},{2,3},{3,4},{4,5},{5,6},{6,7},{7,0},{8,9},{9,10},{10,1... | collective-permute-start | bytes 49160 | tf_op jit(solution)/shard_map/while/body/eval_jaxpr/ppermute | solution.py:26
  318.3 4.5 collective-permute-start
  318.3 7.2 %collective-permute-start.1 = (f32[2,3,2048]{2,1,0:T(4,128)}, f32[2,3,2048]{2,1,0:T(4,128)S(1)}, u32[]{:S(2)}, u32[]{:S(2)}) collective-permute-start(f32[2,3,2048]{2,1,0:T(4,128)} %get-tuple-element.475), channel_id=1, source_target_pairs={{0,1},{1,2},{2,3},{3,4},{4,5},{5,6},{6,7},{7,0},{8,9},{9,10},{10,1... | collective-permute-start | bytes 147464 | tf_op jit(solution)/shard_map/while/body/eval_jaxpr/ppermute | solution.py:26
  328.3 10.7 %collective-permute-start.2 = (f32[2,32,2048]{2,1,0:T(8,128)}, f32[2,32,2048]{2,1,0:T(8,128)S(1)}, u32[]{:S(2)}, u32[]{:S(2)}) collective-permute-start(f32[2,32,2048]{2,1,0:T(8,128)} %fusion.92), channel_id=1, source_target_pairs={{0,8},{8,16},{16,24},{1,9},{9,17},{17,25},{2,10},{10,18},{18,26},{... | collective-permute-start | bytes 1572872 | tf_op jit(solution)/shard_map/while/body/eval_jaxpr/ppermute | solution.py:37
  339.0 3.8 collective-permute-start.3
  339.1 6.5 %collective-permute-start.4 = (f32[2,1,2048]{2,1,0:T(1,128)S(1)}, f32[2,1,2048]{2,1,0:T(1,128)S(1)}, u32[]{:S(2)}, u32[]{:S(2)}) collective-permute-start(f32[2,1,2048]{2,1,0:T(1,128)S(1)} %get-tuple-element.487), channel_id=1, source_target_pairs={{0,1},{1,2},{2,3},{3,4},{4,5},{5,6},{6,7},{7,0},{8,9},{9,10},{10,1... | collective-permute-start | bytes 49160 | tf_op jit(solution)/shard_map/while/body/eval_jaxpr/ppermute | solution.py:26
  358.6 4.5 collective-permute-start
  358.6 7.2 %collective-permute-start.1 = (f32[2,3,2048]{2,1,0:T(4,128)}, f32[2,3,2048]{2,1,0:T(4,128)S(1)}, u32[]{:S(2)}, u32[]{:S(2)}) collective-permute-start(f32[2,3,2048]{2,1,0:T(4,128)} %get-tuple-element.475), channel_id=1, source_target_pairs={{0,1},{1,2},{2,3},{3,4},{4,5},{5,6},{6,7},{7,0},{8,9},{9,10},{10,1... | collective-permute-start | bytes 147464 | tf_op jit(solution)/shard_map/while/body/eval_jaxpr/ppermute | solution.py:26
  368.6 10.7 %collective-permute-start.2 = (f32[2,32,2048]{2,1,0:T(8,128)}, f32[2,32,2048]{2,1,0:T(8,128)S(1)}, u32[]{:S(2)}, u32[]{:S(2)}) collective-permute-start(f32[2,32,2048]{2,1,0:T(8,128)} %fusion.92), channel_id=1, source_target_pairs={{0,8},{8,16},{16,24},{1,9},{9,17},{17,25},{2,10},{10,18},{18,26},{... | collective-permute-start | bytes 1572872 | tf_op jit(solution)/shard_map/while/body/eval_jaxpr/ppermute | solution.py:37
  379.3 3.8 collective-permute-start.3
  379.4 6.5 %collective-permute-start.4 = (f32[2,1,2048]{2,1,0:T(1,128)S(1)}, f32[2,1,2048]{2,1,0:T(1,128)S(1)}, u32[]{:S(2)}, u32[]{:S(2)}) collective-permute-start(f32[2,1,2048]{2,1,0:T(1,128)S(1)} %get-tuple-element.487), channel_id=1, source_target_pairs={{0,1},{1,2},{2,3},{3,4},{4,5},{5,6},{6,7},{7,0},{8,9},{9,10},{10,1... | collective-permute-start | bytes 49160 | tf_op jit(solution)/shard_map/while/body/eval_jaxpr/ppermute | solution.py:26
  398.8 4.5 collective-permute-start
  398.9 7.2 %collective-permute-start.1 = (f32[2,3,2048]{2,1,0:T(4,128)}, f32[2,3,2048]{2,1,0:T(4,128)S(1)}, u32[]{:S(2)}, u32[]{:S(2)}) collective-permute-start(f32[2,3,2048]{2,1,0:T(4,128)} %get-tuple-element.475), channel_id=1, source_target_pairs={{0,1},{1,2},{2,3},{3,4},{4,5},{5,6},{6,7},{7,0},{8,9},{9,10},{10,1... | collective-permute-start | bytes 147464 | tf_op jit(solution)/shard_map/while/body/eval_jaxpr/ppermute | solution.py:26
  408.8 10.7 %collective-permute-start.2 = (f32[2,32,2048]{2,1,0:T(8,128)}, f32[2,32,2048]{2,1,0:T(8,128)S(1)}, u32[]{:S(2)}, u32[]{:S(2)}) collective-permute-start(f32[2,32,2048]{2,1,0:T(8,128)} %fusion.92), channel_id=1, source_target_pairs={{0,8},{8,16},{16,24},{1,9},{9,17},{17,25},{2,10},{10,18},{18,26},{... | collective-permute-start | bytes 1572872 | tf_op jit(solution)/shard_map/while/body/eval_jaxpr/ppermute | solution.py:37
  419.6 3.8 collective-permute-start.3
  419.6 6.5 %collective-permute-start.4 = (f32[2,1,2048]{2,1,0:T(1,128)S(1)}, f32[2,1,2048]{2,1,0:T(1,128)S(1)}, u32[]{:S(2)}, u32[]{:S(2)}) collective-permute-start(f32[2,1,2048]{2,1,0:T(1,128)S(1)} %get-tuple-element.487), channel_id=1, source_target_pairs={{0,1},{1,2},{2,3},{3,4},{4,5},{5,6},{6,7},{7,0},{8,9},{9,10},{10,1... | collective-permute-start | bytes 49160 | tf_op jit(solution)/shard_map/while/body/eval_jaxpr/ppermute | solution.py:26
  439.1 4.5 collective-permute-start
  439.1 7.2 %collective-permute-start.1 = (f32[2,3,2048]{2,1,0:T(4,128)}, f32[2,3,2048]{2,1,0:T(4,128)S(1)}, u32[]{:S(2)}, u32[]{:S(2)}) collective-permute-start(f32[2,3,2048]{2,1,0:T(4,128)} %get-tuple-element.475), channel_id=1, source_target_pairs={{0,1},{1,2},{2,3},{3,4},{4,5},{5,6},{6,7},{7,0},{8,9},{9,10},{10,1... | collective-permute-start | bytes 147464 | tf_op jit(solution)/shard_map/while/body/eval_jaxpr/ppermute | solution.py:26
  450.1 10.7 %collective-permute-start.2 = (f32[2,32,2048]{2,1,0:T(8,128)}, f32[2,32,2048]{2,1,0:T(8,128)S(1)}, u32[]{:S(2)}, u32[]{:S(2)}) collective-permute-start(f32[2,32,2048]{2,1,0:T(8,128)} %fusion.92), channel_id=1, source_target_pairs={{0,8},{8,16},{16,24},{1,9},{9,17},{17,25},{2,10},{10,18},{18,26},{... | collective-permute-start | bytes 1572872 | tf_op jit(solution)/shard_map/while/body/eval_jaxpr/ppermute | solution.py:37
  460.9 6.5 %collective-permute-start.4 = (f32[2,1,2048]{2,1,0:T(1,128)S(1)}, f32[2,1,2048]{2,1,0:T(1,128)S(1)}, u32[]{:S(2)}, u32[]{:S(2)}) collective-permute-start(f32[2,1,2048]{2,1,0:T(1,128)S(1)} %get-tuple-element.487), channel_id=1, source_target_pairs={{0,1},{1,2},{2,3},{3,4},{4,5},{5,6},{6,7},{7,0},{8,9},{9,10},{10,1... | collective-permute-start | bytes 49160 | tf_op jit(solution)/shard_map/while/body/eval_jaxpr/ppermute | solution.py:26
  480.4 4.5 collective-permute-start
  480.4 7.2 %collective-permute-start.1 = (f32[2,3,2048]{2,1,0:T(4,128)}, f32[2,3,2048]{2,1,0:T(4,128)S(1)}, u32[]{:S(2)}, u32[]{:S(2)}) collective-permute-start(f32[2,3,2048]{2,1,0:T(4,128)} %get-tuple-element.475), channel_id=1, source_target_pairs={{0,1},{1,2},{2,3},{3,4},{4,5},{5,6},{6,7},{7,0},{8,9},{9,10},{10,1... | collective-permute-start | bytes 147464 | tf_op jit(solution)/shard_map/while/body/eval_jaxpr/ppermute | solution.py:26
  491.4 10.7 %collective-permute-start.2 = (f32[2,32,2048]{2,1,0:T(8,128)}, f32[2,32,2048]{2,1,0:T(8,128)S(1)}, u32[]{:S(2)}, u32[]{:S(2)}) collective-permute-start(f32[2,32,2048]{2,1,0:T(8,128)} %fusion.92), channel_id=1, source_target_pairs={{0,8},{8,16},{16,24},{1,9},{9,17},{17,25},{2,10},{10,18},{18,26},{... | collective-permute-start | bytes 1572872 | tf_op jit(solution)/shard_map/while/body/eval_jaxpr/ppermute | solution.py:37
  502.2 6.5 %collective-permute-start.4 = (f32[2,1,2048]{2,1,0:T(1,128)S(1)}, f32[2,1,2048]{2,1,0:T(1,128)S(1)}, u32[]{:S(2)}, u32[]{:S(2)}) collective-permute-start(f32[2,1,2048]{2,1,0:T(1,128)S(1)} %get-tuple-element.487), channel_id=1, source_target_pairs={{0,1},{1,2},{2,3},{3,4},{4,5},{5,6},{6,7},{7,0},{8,9},{9,10},{10,1... | collective-permute-start | bytes 49160 | tf_op jit(solution)/shard_map/while/body/eval_jaxpr/ppermute | solution.py:26
  521.7 4.5 collective-permute-start
  521.7 7.2 %collective-permute-start.1 = (f32[2,3,2048]{2,1,0:T(4,128)}, f32[2,3,2048]{2,1,0:T(4,128)S(1)}, u32[]{:S(2)}, u32[]{:S(2)}) collective-permute-start(f32[2,3,2048]{2,1,0:T(4,128)} %get-tuple-element.475), channel_id=1, source_target_pairs={{0,1},{1,2},{2,3},{3,4},{4,5},{5,6},{6,7},{7,0},{8,9},{9,10},{10,1... | collective-permute-start | bytes 147464 | tf_op jit(solution)/shard_map/while/body/eval_jaxpr/ppermute | solution.py:26
  532.7 10.7 %collective-permute-start.2 = (f32[2,32,2048]{2,1,0:T(8,128)}, f32[2,32,2048]{2,1,0:T(8,128)S(1)}, u32[]{:S(2)}, u32[]{:S(2)}) collective-permute-start(f32[2,32,2048]{2,1,0:T(8,128)} %fusion.92), channel_id=1, source_target_pairs={{0,8},{8,16},{16,24},{1,9},{9,17},{17,25},{2,10},{10,18},{18,26},{... | collective-permute-start | bytes 1572872 | tf_op jit(solution)/shard_map/while/body/eval_jaxpr/ppermute | solution.py:37
  543.5 6.5 %collective-permute-start.4 = (f32[2,1,2048]{2,1,0:T(1,128)S(1)}, f32[2,1,2048]{2,1,0:T(1,128)S(1)}, u32[]{:S(2)}, u32[]{:S(2)}) collective-permute-start(f32[2,1,2048]{2,1,0:T(1,128)S(1)} %get-tuple-element.487), channel_id=1, source_target_pairs={{0,1},{1,2},{2,3},{3,4},{4,5},{5,6},{6,7},{7,0},{8,9},{9,10},{10,1... | collective-permute-start | bytes 49160 | tf_op jit(solution)/shard_map/while/body/eval_jaxpr/ppermute | solution.py:26
  (8 other events, 43.8 us)
where the time goes:
time: 555 us; the launch traced here: 551 us
  waiting for transfers between devices  208 us (37%)
  other arithmetic  136 us (25%)
  starting transfers between devices  82.8 us (15%)
  matrix products  81.1 us (15%)
  local copies, waits for them, and re-layouts  41.3 us (7%)
    ppermute x13, waiting for transfers between devices, from_behind(): return lax.ppermute(block, axis, route)  99.8 us
    dot_general x13, matrix products, advance(): jnp.einsum('m,mfij->fij', weights, lap_buf + rea_buf, precision=lax.Preci...  81.1 us
    ppermute x27, waiting for transfers between devices, padded_2(): lax.ppermute(lax.slice_in_dim(block, block.shape[dim] - width, None, axis...  72.9 us
    ppermute x27, starting transfers between devices, padded_2(): lax.ppermute(lax.slice_in_dim(block, block.shape[dim] - width, None, axis...  52.2 us
    ppermute x27, waiting for transfers between devices, padded_2(): lax.ppermute(lax.slice_in_dim(block, 0, width, axis=dim), axis, backward)  35.6 us
    add x13, other arithmetic, advance(): lap_buf + rea_buf  28.7 us
    ppermute x13, starting transfers between devices, from_behind(): return lax.ppermute(block, axis, route)  24.8 us
    select_n x13, other arithmetic, advance(): new_state = jnp.where(active, solved, state)  23.6 us
  transfers between devices with their start and end apart: 67, of which 65 were waited for; matrix products, arithmetic and copies ran while one was open for 7% of the time, Pallas kernels for 0%

commit v1 on v0

v1 whole, which is shorter than its diff:
```python
import functools

import jax
import jax.numpy as jnp
from jax import lax
from jax.experimental import pallas as pl
from jax.experimental.pallas import tpu as pltpu
from jax.sharding import PartitionSpec as P

STEPS = 4
SWEEPS = 3
LANES = 128
SUB = 8
HALF = LANES // 2
FAR = 16
CHUNK = 3

DIFF = (1.0, 0.5)
INV = tuple(1.0 / (1.0 + 4.0 * d) for d in DIFF)
GAIN = tuple(d / (1.0 + 4.0 * d) for d in DIFF)
W = [
    [9.0, 19.0, -5.0, 1.0, 0.0],
    [-1.0, 13.0, 13.0, -1.0, 0.0],
    [1.0, -5.0, 19.0, 9.0, 0.0],
    [0.0, 1.0, -5.0, 19.0, 9.0],
]
MESH = pl.DeviceIdType.MESH


def kernel(
    levels, spaces, tiles, start, u_ref, v_ref, f_ref, k_ref, out_ref,
    send, grid_in, feed, drain, y, lap, rea, corr, rhs, za, zb, nat, pack, recv,
    g_send, g_recv, o_send, o_recv, loc_sem,
):
    lev = lax.axis_index("level")
    spc = lax.axis_index("space")
    rows, width = u_ref.shape
    all_tiles = width // LANES
    pairs = spaces // 2
    pair, side = spc // 2, lax.rem(spc, 2)
    block_tiles = all_tiles // (2 * levels)
    win = block_tiles + 1
    nxt = lax.rem(pair + 1, pairs)
    prv = lax.rem(pair + pairs - 1, pairs)
    block = 2 * lev + side
    own_lo = FAR + rows

    for q, ref in enumerate((u_ref, v_ref, f_ref, k_ref)):
        for j in range(all_tiles + 1):
            jj = j % all_tiles
            send[j, q] = ref[:, jj * LANES : (jj + 1) * LANES]

    barrier = pltpu.get_barrier_semaphore()
    count = 0
    for p in (nxt, prv):
        for s in range(2):
            pl.semaphore_signal(barrier, inc=1, device_id=(lev, 2 * p + s), device_id_type=MESH)
            count += 1
    for dl in range(levels):
        for ds in range(2):
            if dl == 0 and ds == 0:
                continue
            pl.semaphore_signal(
                barrier, inc=1,
                device_id=(lax.rem(lev + dl, levels), 2 * pair + lax.rem(side + ds, 2)),
                device_id_type=MESH,
            )
            count += 1
    pl.semaphore_wait(barrier, count)

    def remote(win_side, r0, n, d0, sem, target, slot):
        return pltpu.make_async_remote_copy(
            src_ref=send.at[pl.ds(block_tiles * (2 * lev + win_side), win), :, pl.ds(r0, n), :],
            dst_ref=grid_in.at[:, :, pl.ds(d0, n), :],
            send_sem=g_send.at[slot], recv_sem=g_recv.at[sem],
            device_id=(lev, target), device_id_type=MESH,
        )

    def gather_copies(s):
        copies = [remote(1 - s, 0, rows, own_lo + rows * s, 0, 2 * pair + 1 - s, 0)]
        for i, t in enumerate((s, 1 - s)):
            if s == 0:
                copies.append(remote(t, rows - FAR, FAR, 0, 1, 2 * nxt + t, 1 + i))
                copies.append(remote(t, 0, rows, own_lo + 2 * rows, 3, 2 * prv + t, 3 + i))
            else:
                copies.append(remote(t, 0, rows, FAR, 2, 2 * nxt + t, 1 + i))
                copies.append(remote(t, 0, FAR, own_lo + 3 * rows, 4, 2 * prv + t, 3 + i))
        return copies

    for s in range(2):
        @pl.when(side == s)
        def _(s=s):
            for c in gather_copies(s):
                c.start()
    own = pltpu.make_async_copy(
        send.at[pl.ds(block_tiles * block, win)],
        grid_in.at[:, :, pl.ds(pl.multiple_of(own_lo + rows * side, SUB), rows), :],
        loc_sem.at[0],
    )
    own.start()
    own.wait()
    for sem, n, d0 in (
        (1, FAR, 0), (2, rows, FAR), (3, rows, own_lo + 2 * rows), (4, FAR, own_lo + 3 * rows)
    ):
        remote(0, 0, n, d0, sem, 2 * nxt, 0).wait_recv()
    remote(0, 0, rows, pl.multiple_of(own_lo + rows * (1 - side), SUB), 0, 2 * nxt, 0).wait_recv()
    for s in range(2):
        @pl.when(side == s)
        def _(s=s):
            for c in gather_copies(s):
                c.wait_send()

    chunks = [(a, min(a + CHUNK, tiles)) for a in range(0, tiles, CHUNK)]
    wide = win * LANES

    def put(ref, q, a, b, val):
        ref[q, a + 1 : b + 1] = val
        if a == 0:
            ref[q, tiles + 1] = pltpu.roll(val[0], SUB - 1, 0)
        if b == tiles:
            ref[q, 0] = pltpu.roll(val[b - a - 1], 1, 0)

    def around(ref, q, a, b):
        mid = ref[q, a + 1 : b + 1]
        flat = mid.reshape((b - a) * SUB, wide)
        cols = pltpu.roll(flat, 1, 1) + pltpu.roll(flat, wide - 1, 1)
        return (ref[q, a:b] + ref[q, a + 2 : b + 2]) + cols.reshape(b - a, SUB, wide), mid

    def rates(node):
        for a, b in chunks:
            nu, u = around(y.at[node], 0, a, b)
            nv, v = around(y.at[node], 1, a, b)
            lap[node, 0, a:b] = DIFF[0] * (nu - 4.0 * u)
            lap[node, 1, a:b] = DIFF[1] * (nv - 4.0 * v)
            uvv = u * v * v
            rea[node, 0, a:b] = feed[a:b] * (1.0 - u) - uvv
            rea[node, 1, a:b] = uvv - drain[a:b] * v

    for t in range(tiles):
        def window(q, t=t):
            return jnp.concatenate(
                [grid_in[j, q, pl.ds(start + t, SUB, stride=tiles), :] for j in range(win)], axis=1
            )
        fd = window(2)
        feed[t] = fd
        drain[t] = fd + window(3)
        for q in range(2):
            put(y.at[0], q, t, t + 1, window(q)[None])
    rates(0)

    def section(n, corrected):
        for q in range(2):
            for a, b in chunks:
                src = y[n, q, a + 1 : b + 1] + rea[n, q, a:b]
                if corrected:
                    src = src + corr[n, q, a:b]
                put(rhs, q, a, b, src * INV[q])
        for old, new, coef in ((rhs, za, DIFF), (za, zb, GAIN), (zb, y.at[n + 1], GAIN)):
            for q in range(2):
                for a, b in chunks:
                    total, _ = around(old, q, a, b)
                    put(new, q, a, b, rhs[q, a + 1 : b + 1] + coef[q] * total)
        rates(n + 1)

    def out_copy(level, s):
        return pltpu.make_async_remote_copy(
            src_ref=pack.at[level, s], dst_ref=recv.at[block],
            send_sem=o_send.at[level, s], recv_sem=o_recv.at[block],
            device_id=(level, 2 * pair + s), device_id_type=MESH,
        )

    low = lax.broadcasted_iota(jnp.int32, (2 * rows, LANES), 1) < HALF

    def emit(level):
        for q in range(2):
            for t in range(tiles):
                row = y[STEPS, q, t + 1]
                for j in range(win):
                    nat[j, q, pl.ds(start + t, SUB, stride=tiles), :] = row[:, j * LANES : (j + 1) * LANES]
            for j in range(block_tiles):
                val = nat[j, q, own_lo : own_lo + 2 * rows]
                if j == 0:
                    val = jnp.where(low, nat[block_tiles, q, own_lo : own_lo + 2 * rows], val)
                for s in range(2):
                    pack[level, s, j, q] = val[s * rows : (s + 1) * rows]
        for s in range(2):
            mine = (level == lev) & (side == s)

            @pl.when(mine)
            def _(s=s):
                pltpu.make_async_copy(pack.at[level, s], recv.at[block], loc_sem.at[1]).start()

            @pl.when(jnp.logical_not(mine))
            def _(s=s):
                out_copy(level, s).start()

    def step0(n, c):
        section(n, False)
        return c

    lax.fori_loop(0, STEPS, step0, 0)
    emit(0)

    def one_level(level, c):
        def correction(t, c):
            for q in range(2):
                laps = [lap[m, q, t] for m in range(STEPS + 1)]
                reas = [rea[m, q, t] for m in range(STEPS + 1)]
                both = [a + b for a, b in zip(laps, reas)]
                for n in range(STEPS):
                    acc = None
                    for m in range(STEPS + 1):
                        if W[n][m] != 0.0:
                            term = (W[n][m] / 24.0) * both[m]
                            acc = term if acc is None else acc + term
                    corr[n, q, t] = acc - laps[n + 1] - reas[n]
            return c

        lax.fori_loop(0, tiles, correction, 0)

        def step(n, c):
            section(n, True)
            return c

        lax.fori_loop(0, STEPS, step, 0)
        emit(level)
        return c

    lax.fori_loop(1, levels, one_level, 0)

    for level in range(levels):
        for s in range(2):
            mine = (lev == level) & (side == s)

            @pl.when(mine)
            def _(level=level, s=s):
                pltpu.make_async_copy(pack.at[level, s], recv.at[block], loc_sem.at[1]).wait()

            @pl.when(jnp.logical_not(mine))
            def _(level=level, s=s):
                out_copy(level, s).wait_send()
    for b in range(2 * levels):
        @pl.when(block != b)
        def _(b=b):
            pltpu.make_async_remote_copy(
                src_ref=pack.at[0, 0], dst_ref=recv.at[b],
                send_sem=o_send.at[0, 0], recv_sem=o_recv.at[b],
                device_id=(lev, 2 * pair + 1 - side), device_id_type=MESH,
            ).wait_recv()
    low1 = lax.broadcasted_iota(jnp.int32, (rows, LANES), 1) < HALF
    for b in range(2 * levels):
        before = (b + 2 * levels - 1) % (2 * levels)
        for q in range(2):
            for j in range(block_tiles):
                val = recv[b, j, q]
                if j == 0:
                    val = jnp.where(low1, recv[before, 0, q], val)
                at = (b * block_tiles + j) * LANES
                out_ref[0, q, :, at : at + LANES] = val


def body(u_init, v_init, feed_rate, kill_rate):
    rows, width = u_init.shape
    levels = lax.axis_size("level")
    spaces = lax.axis_size("space")
    block_tiles = width // LANES // (2 * levels)
    win = block_tiles + 1
    wide = win * LANES
    tall = 4 * rows + 2 * FAR
    need = STEPS * SWEEPS + (levels - 1) * (SWEEPS * (STEPS - 1) + 1)
    tiles = -(-(2 * rows + 2 * need) // SUB)
    start = (tall - tiles * SUB) // 2
    assert start >= 0 and need <= HALF
    f32 = jnp.float32
    ghost = (2, tiles + 2, SUB, wide)
    plain = (2, tiles, SUB, wide)
    scratch = [
        pltpu.VMEM((width // LANES + 1, 4, rows, LANES), f32),
        pltpu.VMEM((win, 4, tall, LANES), f32),
        pltpu.VMEM(plain[1:], f32),
        pltpu.VMEM(plain[1:], f32),
        pltpu.VMEM((STEPS + 1,) + ghost, f32),
        pltpu.VMEM((STEPS + 1,) + plain, f32),
        pltpu.VMEM((STEPS + 1,) + plain, f32),
        pltpu.VMEM((STEPS,) + plain, f32),
        pltpu.VMEM(ghost, f32),
        pltpu.VMEM(ghost, f32),
        pltpu.VMEM(ghost, f32),
        pltpu.VMEM((win, 2, tall, LANES), f32),
        pltpu.VMEM((levels, 2, block_tiles, 2, rows, LANES), f32),
        pltpu.VMEM((2 * levels, block_tiles, 2, rows, LANES), f32),
        pltpu.SemaphoreType.DMA((5,)),
        pltpu.SemaphoreType.DMA((5,)),
        pltpu.SemaphoreType.DMA((levels, 2)),
        pltpu.SemaphoreType.DMA((2 * levels,)),
        pltpu.SemaphoreType.DMA((2,)),
    ]
    return pl.pallas_call(
        functools.partial(kernel, levels, spaces, tiles, start),
        out_shape=jax.ShapeDtypeStruct((1, 2, rows, width), f32),
        in_specs=[pl.BlockSpec(memory_space=pltpu.VMEM)] * 4,
        out_specs=pl.BlockSpec(memory_space=pltpu.VMEM),
        scratch_shapes=scratch,
        compiler_params=pltpu.CompilerParams(
            collective_id=0, has_side_effects=True, vmem_limit_bytes=56 * 1024 * 1024
        ),
    )(u_init, v_init, feed_rate, kill_rate)


def solution(mesh):
    return jax.shard_map(
        body,
        mesh=mesh,
        in_specs=(P("space", None),) * 4,
        out_specs=P("level", None, "space", None),
        check_vma=False,
    )
```

time: 555 us -> 47 us (0.08)
  the two profiles are of different devices: /device:TPU:2 before, /device:TPU:0 now
where the time goes in v1:
time: 47 us; the launch traced here: 46.8 us
  Pallas kernels  44.9 us (96%)
  local copies, waits for them, and re-layouts  1.87 us (4%)
    pallas_call x1, Pallas kernels, body(): pl.pallas_call(functools.partial(kernel, levels, spaces, tiles, start), o...  44.9 us
    unnamed x1, local copies, waits for them, and re-layouts  1.87 us

profile of v1, /device:TPU:0, one launch (start us, length us, event | category | flops | bytes accessed | tf_op | source)
XLA Modules:
  0.0 46.8 jit_solution(10109228290447367870)
XLA Ops:
  0.0 44.9 %shard_map.46 = f32[1,2,32,2048]{3,2,1,0:T(8,128)} custom-call(f32[32,2048]{1,0:T(8,128)} %u_ref.1, f32[32,2048]{1,0:T(8,128)} %v_ref.1, f32[32,2048]{1,0:T(8,128)} %f_ref.1, f32[32,2048]{1,0:T(8,128)} %k_ref.1), custom_call_target="tpu_custom_call" | custom-call | tf_op jit(solution)/shard_map/pallas_call | solution.py:298
  44.9 1.9 %copy.6 = f32[1,2,32,2048]{3,2,1,0:T(8,128)} copy(f32[1,2,32,2048]{3,2,1,0:T(8,128)} %shard_map.46) | data formatting | bytes 1048576

commit v2 on v1

--- a/solution.py
+++ b/solution.py
@@ -28,8 +28,8 @@
 
 
 def kernel(
-    levels, spaces, tiles, start, u_ref, v_ref, f_ref, k_ref, out_ref,
-    send, grid_in, feed, drain, y, lap, rea, corr, rhs, za, zb, nat, pack, recv,
+    levels, spaces, level_tiles, tall, u_ref, v_ref, f_ref, k_ref, out_ref,
+    send, grid_in, feed, drain, y, lap, rea, corr, rhs, za, zb, nat, cnat, pack, recv,
     g_send, g_recv, o_send, o_recv, loc_sem,
 ):
     lev = lax.axis_index("level")
@@ -110,10 +110,9 @@
             for c in gather_copies(s):
                 c.wait_send()
 
-    chunks = [(a, min(a + CHUNK, tiles)) for a in range(0, tiles, CHUNK)]
     wide = win * LANES
 
-    def put(ref, q, a, b, val):
+    def put(tiles, ref, q, a, b, val):
         ref[q, a + 1 : b + 1] = val
         if a == 0:
             ref[q, tiles + 1] = pltpu.roll(val[0], SUB - 1, 0)
@@ -126,41 +125,50 @@
         cols = pltpu.roll(flat, 1, 1) + pltpu.roll(flat, wide - 1, 1)
         return (ref[q, a:b] + ref[q, a + 2 : b + 2]) + cols.reshape(b - a, SUB, wide), mid
 
-    def rates(node):
-        for a, b in chunks:
+    def rates(tiles, node, last=False):
+        for a, b in chunks_of(tiles):
             nu, u = around(y.at[node], 0, a, b)
             nv, v = around(y.at[node], 1, a, b)
-            lap[node, 0, a:b] = DIFF[0] * (nu - 4.0 * u)
-            lap[node, 1, a:b] = DIFF[1] * (nv - 4.0 * v)
+            if not last:
+                lap[node, 0, a:b] = DIFF[0] * (nu - 4.0 * u)
+                lap[node, 1, a:b] = DIFF[1] * (nv - 4.0 * v)
             uvv = u * v * v
             rea[node, 0, a:b] = feed[a:b] * (1.0 - u) - uvv
             rea[node, 1, a:b] = uvv - drain[a:b] * v
 
-    for t in range(tiles):
-        def window(q, t=t):
-            return jnp.concatenate(
-                [grid_in[j, q, pl.ds(start + t, SUB, stride=tiles), :] for j in range(win)], axis=1
-            )
-        fd = window(2)
-        feed[t] = fd
-        drain[t] = fd + window(3)
+    def setup(tiles, corrected, last):
+        start = (tall - tiles * SUB) // 2
+        for t in range(tiles):
+            def window(ref, t=t):
+                return jnp.concatenate(
+                    [ref(j)[pl.ds(start + t, SUB, stride=tiles), :] for j in range(win)], axis=1
+                )
+            fd = window(lambda j: grid_in.at[j, 2])
+            feed[t] = fd
+            drain[t] = fd + window(lambda j: grid_in.at[j, 3])
+            for q in range(2):
+                put(tiles, y.at[0], q, t, t + 1, window(lambda j, q=q: grid_in.at[j, q])[None])
+                if corrected:
+                    for n in range(STEPS):
+                        corr[n, q, t] = window(lambda j, q=q, n=n: cnat.at[n, q, j])
+        rates(tiles, 0, last)
+
+    def chunks_of(tiles):
+        return [(a, min(a + CHUNK, tiles)) for a in range(0, tiles, CHUNK)]
+
+    def section(tiles, n, corrected, last):
         for q in range(2):
-            put(y.at[0], q, t, t + 1, window(q)[None])
-    rates(0)
-
-    def section(n, corrected):
-        for q in range(2):
-            for a, b in chunks:
+            for a, b in chunks_of(tiles):
                 src = y[n, q, a + 1 : b + 1] + rea[n, q, a:b]
                 if corrected:
                     src = src + corr[n, q, a:b]
-                put(rhs, q, a, b, src * INV[q])
+                put(tiles, rhs, q, a, b, src * INV[q])
         for old, new, coef in ((rhs, za, DIFF), (za, zb, GAIN), (zb, y.at[n + 1], GAIN)):
             for q in range(2):
-                for a, b in chunks:
+                for a, b in chunks_of(tiles):
                     total, _ = around(old, q, a, b)
-                    put(new, q, a, b, rhs[q, a + 1 : b + 1] + coef[q] * total)
-        rates(n + 1)
+                    put(tiles, new, q, a, b, rhs[q, a + 1 : b + 1] + coef[q] * total)
+        rates(tiles, n + 1, last)
 
     def out_copy(level, s):
         return pltpu.make_async_remote_copy(
@@ -171,7 +179,8 @@
 
     low = lax.broadcasted_iota(jnp.int32, (2 * rows, LANES), 1) < HALF
 
-    def emit(level):
+    def emit(tiles, level):
+        start = (tall - tiles * SUB) // 2
         for q in range(2):
             for t in range(tiles):
                 row = y[STEPS, q, t + 1]
@@ -194,39 +203,36 @@
             def _(s=s):
                 out_copy(level, s).start()
 
-    def step0(n, c):
-        section(n, False)
-        return c
-
-    lax.fori_loop(0, STEPS, step0, 0)
-    emit(0)
-
-    def one_level(level, c):
-        def correction(t, c):
+    def correct(tiles):
+        start = (tall - tiles * SUB) // 2
+        for t in range(tiles):
             for q in range(2):
                 laps = [lap[m, q, t] for m in range(STEPS + 1)]
                 reas = [rea[m, q, t] for m in range(STEPS + 1)]
                 both = [a + b for a, b in zip(laps, reas)]
                 for n in range(STEPS):
-                    acc = None
+                    acc = -laps[n + 1] - reas[n]
                     for m in range(STEPS + 1):
                         if W[n][m] != 0.0:
-                            term = (W[n][m] / 24.0) * both[m]
-                            acc = term if acc is None else acc + term
-                    corr[n, q, t] = acc - laps[n + 1] - reas[n]
+                            acc = acc + (W[n][m] / 24.0) * both[m]
+                    for j in range(win):
+                        cnat[n, q, j, pl.ds(start + t, SUB, stride=tiles), :] = acc[
+                            :, j * LANES : (j + 1) * LANES
+                        ]
+
+    for level in range(levels):
+        tiles = level_tiles[level]
+        last = level == levels - 1
+        setup(tiles, level > 0, last)
+
+        def step(n, c, tiles=tiles, level=level, last=last):
+            section(tiles, n, level > 0, last)
             return c
 
-        lax.fori_loop(0, tiles, correction, 0)
-
-        def step(n, c):
-            section(n, True)
-            return c
-
         lax.fori_loop(0, STEPS, step, 0)
-        emit(level)
-        return c
-
-    lax.fori_loop(1, levels, one_level, 0)
+        emit(tiles, level)
+        if not last:
+            correct(tiles)
 
     for level in range(levels):
         for s in range(2):
@@ -267,10 +273,12 @@
     win = block_tiles + 1
     wide = win * LANES
     tall = 4 * rows + 2 * FAR
-    need = STEPS * SWEEPS + (levels - 1) * (SWEEPS * (STEPS - 1) + 1)
-    tiles = -(-(2 * rows + 2 * need) // SUB)
-    start = (tall - tiles * SUB) // 2
-    assert start >= 0 and need <= HALF
+    needs = [
+        STEPS * SWEEPS + (levels - 1 - k) * (SWEEPS * (STEPS - 1) + 1) for k in range(levels)
+    ]
+    level_tiles = [-(-(2 * rows + 2 * need) // SUB) for need in needs]
+    tiles = level_tiles[0]
+    assert tiles * SUB <= tall and needs[0] <= HALF
     f32 = jnp.float32
     ghost = (2, tiles + 2, SUB, wide)
     plain = (2, tiles, SUB, wide)
@@ -287,6 +295,7 @@
         pltpu.VMEM(ghost, f32),
         pltpu.VMEM(ghost, f32),
         pltpu.VMEM((win, 2, tall, LANES), f32),
+        pltpu.VMEM((STEPS, 2, win, tall, LANES), f32),
         pltpu.VMEM((levels, 2, block_tiles, 2, rows, LANES), f32),
         pltpu.VMEM((2 * levels, block_tiles, 2, rows, LANES), f32),
         pltpu.SemaphoreType.DMA((5,)),
@@ -296,7 +305,7 @@
         pltpu.SemaphoreType.DMA((2,)),
     ]
     return pl.pallas_call(
-        functools.partial(kernel, levels, spaces, tiles, start),
+        functools.partial(kernel, levels, spaces, level_tiles, tall),
         out_shape=jax.ShapeDtypeStruct((1, 2, rows, width), f32),
         in_specs=[pl.BlockSpec(memory_space=pltpu.VMEM)] * 4,
         out_specs=pl.BlockSpec(memory_space=pltpu.VMEM),

time: 47 us -> 44.2 us (0.940)
  Pallas kernels: 44.9 us -> 42.1 us
    pallas_call x1, Pallas kernels: 44.9 us -> 42.1 us  [body(): pl.pallas_call(functools.partial(kernel, levels, spaces, level_tiles, tal...]
where the time goes in v2:
time: 44.2 us; the launch traced here: 44 us
  Pallas kernels  42.1 us (95%)
  local copies, waits for them, and re-layouts  1.87 us (4%)
    pallas_call x1, Pallas kernels, body(): pl.pallas_call(functools.partial(kernel, levels, spaces, level_tiles, tal...  42.1 us
    unnamed x1, local copies, waits for them, and re-layouts  1.87 us

profile of v2, /device:TPU:0, one launch (start us, length us, event | category | flops | bytes accessed | tf_op | source)
XLA Modules:
  0.0 44.0 jit_solution(11292027206861150164)
XLA Ops:
  0.0 42.1 %shard_map.46 = f32[1,2,32,2048]{3,2,1,0:T(8,128)} custom-call(f32[32,2048]{1,0:T(8,128)} %u_ref.1, f32[32,2048]{1,0:T(8,128)} %v_ref.1, f32[32,2048]{1,0:T(8,128)} %f_ref.1, f32[32,2048]{1,0:T(8,128)} %k_ref.1), custom_call_target="tpu_custom_call" | custom-call | tf_op jit(solution)/shard_map/pallas_call | solution.py:307
  42.1 1.9 %copy.6 = f32[1,2,32,2048]{3,2,1,0:T(8,128)} copy(f32[1,2,32,2048]{3,2,1,0:T(8,128)} %shard_map.46) | data formatting | bytes 1048576

commit v3 on v2

--- a/solution.py
+++ b/solution.py
@@ -12,7 +12,7 @@
 LANES = 128
 SUB = 8
 HALF = LANES // 2
-FAR = 16
+FAR = 12
 CHUNK = 3
 
 DIFF = (1.0, 0.5)
@@ -94,7 +94,7 @@
                 c.start()
     own = pltpu.make_async_copy(
         send.at[pl.ds(block_tiles * block, win)],
-        grid_in.at[:, :, pl.ds(pl.multiple_of(own_lo + rows * side, SUB), rows), :],
+        grid_in.at[:, :, pl.ds(pl.multiple_of(own_lo + rows * side, 4), rows), :],
         loc_sem.at[0],
     )
     own.start()
@@ -103,7 +103,7 @@
         (1, FAR, 0), (2, rows, FAR), (3, rows, own_lo + 2 * rows), (4, FAR, own_lo + 3 * rows)
     ):
         remote(0, 0, n, d0, sem, 2 * nxt, 0).wait_recv()
-    remote(0, 0, rows, pl.multiple_of(own_lo + rows * (1 - side), SUB), 0, 2 * nxt, 0).wait_recv()
+    remote(0, 0, rows, pl.multiple_of(own_lo + rows * (1 - side), 4), 0, 2 * nxt, 0).wait_recv()
     for s in range(2):
         @pl.when(side == s)
         def _(s=s):

time: 44.2 us -> 43.4 us (0.982)
  Pallas kernels: 42.1 us -> 41.4 us
    pallas_call x1, Pallas kernels: 42.1 us -> 41.4 us  [body(): pl.pallas_call(functools.partial(kernel, levels, spaces, level_tiles, tal...]
where the time goes in v3:
time: 43.4 us; the launch traced here: 43.2 us
  Pallas kernels  41.4 us (95%)
  local copies, waits for them, and re-layouts  1.87 us (4%)
    pallas_call x1, Pallas kernels, body(): pl.pallas_call(functools.partial(kernel, levels, spaces, level_tiles, tal...  41.4 us
    unnamed x1, local copies, waits for them, and re-layouts  1.87 us

profile of v3, /device:TPU:0, one launch (start us, length us, event | category | flops | bytes accessed | tf_op | source)
XLA Modules:
  0.0 43.2 jit_solution(15086551886352362197)
XLA Ops:
  0.0 41.4 %shard_map.46 = f32[1,2,32,2048]{3,2,1,0:T(8,128)} custom-call(f32[32,2048]{1,0:T(8,128)} %u_ref.1, f32[32,2048]{1,0:T(8,128)} %v_ref.1, f32[32,2048]{1,0:T(8,128)} %f_ref.1, f32[32,2048]{1,0:T(8,128)} %k_ref.1), custom_call_target="tpu_custom_call" | custom-call | tf_op jit(solution)/shard_map/pallas_call | solution.py:307
  41.4 1.9 %copy.6 = f32[1,2,32,2048]{3,2,1,0:T(8,128)} copy(f32[1,2,32,2048]{3,2,1,0:T(8,128)} %shard_map.46) | data formatting | bytes 1048576
